TPU v7x, 32 devices: a whole 2x2x4 slice. The times are simulated.
32 devices in a mesh: rows: 8 (over y, x, core), feat: 4 (over z).
Axes of the slice: x: 2, y: 2, z: 4, core: 2. Of those that a mesh axis runs over, the one named last changes fastest.
Arguments:
- features: bfloat16 [8192, 2048], P('rows', 'feat'), may hold values from -6 to 6
- grad_out: bfloat16 [8192, 2048], P('rows', 'feat'), may hold values from -6 to 6
- eigvecs: float32 [2048, 2048], P('feat', 'rows'), may hold values from -1 to 1, as said below
- eigvals: float32 [2048], replicated, may hold values from 0.1 to 1, as said below
- whiten: bfloat16 [2048, 2048], P(None, 'feat'), may hold values from -0.125 to 0.125
Outputs:
- grad_in: bfloat16 [8192, 2048], P('rows', 'feat')
Inputs may be any that keep to these rules, and one draw needn't show every extreme that they name: `eigvecs`: the columns are orthonormal. `eigvals`: any two entries differ by at least 0.45 / 2048.
All inputs are finite; a program needn't handle non-finite values.
Results may differ from a plain program's by a relative error of at most 0.0074.
Values may be sent and summed in bfloat16 or wider, within the bound.
A program may use at most 128 MiB of HBM per device.

v0:
```python
import jax
import jax.numpy as jnp
from jax import lax
from jax.sharding import PartitionSpec as P


def divided(lam_row, lam_col, first_col):
    on_diag = (
        jnp.arange(lam_row.shape[0], dtype=jnp.int32)[:, None]
        == (first_col + jnp.arange(lam_col.shape[0], dtype=jnp.int32))[None, :]
    )
    root_row = lam_row ** (-0.5)
    root_col = lam_col ** (-0.5)
    gaps_lam = lam_row[:, None] - lam_col[None, :]
    safe_gap = jnp.where(on_diag, jnp.ones_like(gaps_lam), gaps_lam)
    off_diag = (root_row[:, None] - root_col[None, :]) / safe_gap
    diag_vals = -0.5 * lam_row[:, None] ** (-1.5) + jnp.zeros_like(gaps_lam)
    return jnp.where(on_diag, diag_vals, off_diag)


def local(features, grad_out, eigvecs, eigvals, whiten):
    highest = lax.Precision.HIGHEST
    tok_rows, own_cols = features.shape
    row_count = tok_rows * lax.axis_size("rows")
    contract_rows = (((0,), (0,)), ((), ()))
    contract_last = (((1,), (1,)), ((), ()))
    piece_x = lax.all_gather(features, "feat", axis=1, tiled=True)
    piece_g = lax.all_gather(grad_out, "feat", axis=1, tiled=True)
    left_part = lax.dot_general(
        features, piece_g, contract_rows, preferred_element_type=jnp.float32
    )
    right_part = lax.dot_general(
        grad_out, piece_x, contract_rows, preferred_element_type=jnp.float32
    )
    cross_one = left_part
    cross_two = right_part
    sum_x = jnp.sum(piece_x, axis=0, dtype=jnp.float32)
    sum_g = jnp.sum(piece_g, axis=0, dtype=jnp.float32)
    cross_one, cross_two, sum_x, sum_g = (cross_one, cross_two, sum_x, sum_g)
    cross_one, cross_two, sum_x, sum_g = lax.psum((cross_one, cross_two, sum_x, sum_g), "rows")
    both_cross = cross_one + cross_two
    col_mean = sum_x / row_count
    grad_mean = sum_g / row_count
    offset = lax.axis_index("feat") * own_cols
    mean_part = lax.dynamic_slice_in_dim(col_mean, offset, own_cols)
    grad_part = lax.dynamic_slice_in_dim(grad_mean, offset, own_cols)
    sym_gram = 0.5 * (
        both_cross
        - row_count
        * (mean_part[:, None] * grad_mean[None, :] + grad_part[:, None] * col_mean[None, :])
    )
    basis_cols = lax.all_gather(eigvecs, "feat", axis=0, tiled=True)
    basis_block = lax.all_gather(eigvecs, "rows", axis=1, tiled=True)
    narrow = basis_cols.shape[1]
    inner_prod = jnp.dot(sym_gram, basis_cols, precision=highest)
    partial_value = lax.dot_general(basis_block, inner_prod, contract_rows, precision=highest)
    rotated = lax.psum(partial_value, "feat")
    first_col = lax.axis_index("rows") * narrow
    lam_col = lax.dynamic_slice_in_dim(eigvals, first_col, narrow)
    scaled = divided(eigvals, lam_col, first_col) * rotated
    back_rot = jnp.dot(basis_block, scaled, precision=highest)
    sens_own = lax.psum_scatter(
        lax.dot_general(back_rot, basis_cols, contract_last, precision=highest),
        "rows",
        scatter_dimension=0,
        tiled=True,
    )
    scaled_own = (2.0 / row_count * sens_own).astype(jnp.bfloat16)
    sens_scaled = lax.all_gather(scaled_own, "rows", axis=0, tiled=True)
    piece_x = lax.all_gather(features, "feat", axis=1, tiled=True)
    piece_g = lax.all_gather(grad_out, "feat", axis=1, tiled=True)
    shifted = (piece_g.astype(jnp.float32) - grad_mean).astype(jnp.bfloat16)
    centered = (piece_x.astype(jnp.float32) - col_mean).astype(jnp.bfloat16)
    running = jnp.dot(shifted, whiten, preferred_element_type=jnp.float32)
    grad_in = running + lax.dot_general(
        centered, sens_scaled, contract_last, preferred_element_type=jnp.float32
    )
    return grad_in.astype(jnp.bfloat16)


def solution(mesh):
    in_specs = (P("rows", "feat"), P("rows", "feat"), P("feat", "rows"), P(), P(None, "feat"))
    out_specs = P("rows", "feat")
    return jax.shard_map(local, mesh=mesh, in_specs=in_specs, out_specs=out_specs, check_vma=False)
```

profile of v0, /device:TPU:0, one launch (start us, length us, event | category | flops | bytes accessed | tf_op | source)
XLA Modules:
  0.0 552.3 jit_solution(13871746332786428748)
XLA Ops:
  6.5 0.7 all-gather.6.cloned.1.call-update
  7.3 0.7 all-gather.8.cloned.1.call-update
  8.1 0.7 all-gather.10.cloned.1.call-update
  8.8 83.6 %all-gather.6.cloned.1.call-done = bf16[1024,2048]{1,0:T(8,128)(2,1)} async-done(((bf16[1024,512]{1,0:T(8,128)(2,1)}), bf16[1024,2048]{1,0:T(8,128)(2,1)}) %all-gather.6.cloned.1.call-update) | async-done | bytes 4194320 | tf_op jit(solution)/shard_map/all_gather | solution.py:71
  92.4 6.8 %fusion.40 = f32[512,2048]{1,0:T(8,128)} fusion(bf16[1024,512]{1,0:T(8,128)(2,1)} %param.5, bf16[1024,2048]{1,0:T(8,128)(2,1)} %all-gather.6.cloned.1.call-done), kind=kOutput, calls=%fused_computation.51 | convolution fusion | flops 2147483648 | bytes 9437184 | tf_op jit(solution)/shard_map/dot_general | solution.py:29
  99.2 74.0 %all-gather.8.cloned.1.call-done = bf16[1024,2048]{1,0:T(8,128)(2,1)} async-done(((bf16[1024,512]{1,0:T(8,128)(2,1)}), bf16[1024,2048]{1,0:T(8,128)(2,1)}) %all-gather.8.cloned.1.call-update) | async-done | bytes 4194320 | tf_op jit(solution)/shard_map/all_gather | solution.py:70
  173.2 7.8 %convolution_add_fusion = f32[512,2048]{1,0:T(8,128)} fusion(f32[512,2048]{1,0:T(8,128)} %fusion.40, bf16[1024,512]{1,0:T(8,128)(2,1)S(1)} %copy-done.3, bf16[1024,2048]{1,0:T(8,128)(2,1)} %all-gather.8.cloned.1.call-done), kind=kOutput, calls=%fused_computation.17 | convolution fusion | flops 2148532224 | bytes 13631488 | tf_op jit(solution)/shard_map/dot_general | solution.py:32
  181.1 0.5 all-gather.12.cloned.1.call-update
  181.7 3.0 convert_reduce_fusion
  185.2 0.6 convert_reduce_fusion.1
  185.8 25.6 %all-reduce = (f32[2048]{0:T(1024)S(1)}, f32[2048]{0:T(1024)S(1)}) all-reduce(f32[2048]{0:T(1024)S(1)} %convert_reduce_fusion, f32[2048]{0:T(1024)S(1)} %convert_reduce_fusion.1), channel_id=1, replica_groups=mesh['rows'=8,'feat'=4] {'rows'}, use_global_device_ids=true, to_apply=%region_3.0 | all-reduce | flops 4096 | bytes 32768 | tf_op jit(solution)/shard_map/psum | solution.py:40
  211.6 7.4 %all-gather.10.cloned.1.call-done = f32[2048,256]{1,0:T(8,128)} async-done(((f32[512,256]{1,0:T(8,128)}), f32[2048,256]{1,0:T(8,128)}) %all-gather.10.cloned.1.call-update) | async-done | bytes 2097168 | tf_op jit(solution)/shard_map/all_gather | solution.py:52
  219.0 82.8 %all-reduce.6.cloned.1.call-done = f32[512,2048]{1,0:T(8,128)} async-done(((f32[512,2048]{1,0:T(8,128)}), f32[512,2048]{1,0:T(8,128)}) %all-reduce.6.cloned.1.call-update) | async-done | bytes 4194320 | tf_op jit(solution)/shard_map/psum | solution.py:40
  301.7 6.9 %fusion.6 = f32[512,256]{1,0:T(8,128)S(1)} fusion(f32[2048,256]{1,0:T(8,128)} %all-gather.10.cloned.1.call-done, f32[512,2048]{1,0:T(8,128)} %all-reduce.6.cloned.1.call-done, f32[2048]{0:T(1024)S(1)} %get-tuple-element.11, f32[512]{0:T(512)S(1)} %dynamic_slice.11, f32[2048]{0:T(1024)S(1)} %get-tuple-element.12, f32[512]{0:T(512)S(1)} %dynamic_slice.10), kind=kOutput, calls=%fused_computation.8 | convolution fusion | flops 3227516928 | bytes 6836224 | tf_op jit(solution)/shard_map/dot_general | solution.py:55
  308.6 32.3 %all-gather.12.cloned.1.call-done = f32[512,2048]{1,0:T(8,128)} async-done(((f32[512,256]{1,0:T(8,128)}), f32[512,2048]{1,0:T(8,128)}) %all-gather.12.cloned.1.call-update) | async-done | bytes 4194320 | tf_op jit(solution)/shard_map/all_gather | solution.py:53
  340.9 10.2 %convolution_bitcast_fusion = f32[2048,256]{1,0:T(8,128)} fusion(f32[512,256]{1,0:T(8,128)S(1)} %fusion.6, f32[512,2048]{1,0:T(8,128)} %all-gather.12.cloned.1.call-done), kind=kOutput, calls=%fused_computation.18 | convolution fusion | flops 3221225472 | bytes 6815744 | tf_op jit(solution)/shard_map/dot_general | solution.py:56
  351.5 85.9 %all-reduce.4.cloned.1.call-done = f32[2048,256]{1,0:T(8,128)} async-done(((f32[2048,256]{1,0:T(8,128)}), f32[2048,256]{1,0:T(8,128)}) %all-reduce.4.cloned.1.call-update) | async-done | bytes 2097168 | tf_op jit(solution)/shard_map/psum | solution.py:57
  437.4 10.8 %fusion.15 = f32[256,512]{1,0:T(8,128)S(1)} fusion(f32[512,2048]{1,0:T(8,128)} %all-gather.12.cloned.1.call-done, f32[2048,256]{1,0:T(8,128)} %all-reduce.4.cloned.1.call-done, f32[256]{0:T(256)S(1)} %get-tuple-element.8, f32[2048]{0:T(1024)S(1)} %copy-done.5, f32[256]{0:T(256)S(1)} %get-tuple-element.7, f32[2048]{0:T(1024)S(1)} %get-tuple-element.10, ...), kind=kOutput, calls=%fused_computation.20 | convolution fusion | flops 3224895488 | bytes 6843392 | tf_op jit(solution)/shard_map/dot_general | solution.py:61
  448.2 8.4 %fusion.41 = f32[512,2048]{1,0:T(8,128)} fusion(f32[256,512]{1,0:T(8,128)S(1)} %fusion.15, f32[2048,256]{1,0:T(8,128)S(1)} %copy-done.4), kind=kOutput, calls=%fused_computation.52 | convolution fusion | flops 3221225472 | bytes 6815744 | tf_op jit(solution)/shard_map/dot_general | solution.py:63
  457.0 50.0 %reduce-scatter.2.cloned.1.call-done = f32[64,2048]{1,0:T(8,128)} async-done(((f32[512,2048]{1,0:T(8,128)}), f32[64,2048]{1,0:T(8,128)}) %reduce-scatter.2.cloned.1.call-update) | async-done | bytes 524304 | tf_op jit(solution)/shard_map/reduce_scatter | solution.py:62
  507.0 1.8 multiply_convert_fusion
  508.8 27.9 %all-gather.14.cloned.1.call-done = bf16[512,2048]{1,0:T(8,128)(2,1)} async-done(((bf16[64,2048]{1,0:T(8,128)(2,1)}), bf16[512,2048]{1,0:T(8,128)(2,1)}) %all-gather.14.cloned.1.call-update) | async-done | bytes 2097168 | tf_op jit(solution)/shard_map/all_gather | solution.py:69
  536.7 5.4 fusion.2
  542.1 3.3 add_convert_fusion
  (30 shorter events, 1.6 us)
Async XLA Ops:
  6.5 535.6 %copy-start = (bf16[2048,512]{1,0:T(8,128)(2,1)S(1)}, bf16[2048,512]{1,0:T(8,128)(2,1)}, u32[]{:S(2)}) copy-start(bf16[2048,512]{1,0:T(8,128)(2,1)} %param.9) | copy-start | bytes 6291460
  6.5 85.9 %all-gather.6.cloned.1.call-start = ((), (), s32[]{:S(2)}) async-start(), calls=%async_computation.1 | async-start | bytes 5242880 | tf_op jit(solution)/shard_map/all_gather | solution.py:71
  7.3 166.0 %all-gather.8.cloned.1.call-start = ((), (), s32[]{:S(2)}) async-start(), calls=%async_computation.2 | async-start | bytes 5242880 | tf_op jit(solution)/shard_map/all_gather | solution.py:70
  8.0 211.0 %all-gather.10.cloned.1.call-start = ((), (), s32[]{:S(2)}) async-start(), calls=%async_computation.3 | async-start | bytes 2621440 | tf_op jit(solution)/shard_map/all_gather | solution.py:52
  8.7 164.5 %copy-start.3 = (bf16[1024,512]{1,0:T(8,128)(2,1)S(1)}, bf16[1024,512]{1,0:T(8,128)(2,1)}, u32[]{:S(2)}) copy-start(bf16[1024,512]{1,0:T(8,128)(2,1)} %param.6) | copy-start | bytes 3145732
  8.8 293.0 %all-reduce.6.cloned.1.call-start = ((), (), s32[]{:S(2)}) async-start(), calls=%async_computation.8 | async-start | bytes 8388608 | tf_op jit(solution)/shard_map/psum | solution.py:40
  181.1 159.9 %all-gather.12.cloned.1.call-start = ((), (), s32[]{:S(2)}) async-start(), calls=%async_computation.4 | async-start | bytes 4718592 | tf_op jit(solution)/shard_map/all_gather | solution.py:53
  181.7 255.8 %all-reduce.4.cloned.1.call-start = ((), (), s32[]{:S(2)}) async-start(), calls=%async_computation.5 | async-start | bytes 4194304 | tf_op jit(solution)/shard_map/psum | solution.py:57
  181.7 3.5 copy-start.1
  308.6 42.8 %copy-start.5 = (f32[2048]{0:T(1024)S(1)}, f32[2048]{0:T(1024)}, u32[]{:S(2)}) copy-start(f32[2048]{0:T(1024)} %param.8) | copy-start | bytes 24580
  351.1 155.9 %reduce-scatter.2.cloned.1.call-start = ((), (), s32[]{:S(2)}) async-start(), calls=%async_computation.6 | async-start | bytes 4718592 | tf_op jit(solution)/shard_map/reduce_scatter | solution.py:62
  437.4 10.8 %copy-start.4 = (f32[2048,256]{1,0:T(8,128)S(1)}, f32[2048,256]{1,0:T(8,128)}, u32[]{:S(2)}) copy-start(f32[2048,256]{1,0:T(8,128)} %all-gather.10.cloned.1.call-done) | copy-start | bytes 6291460
  456.7 80.1 %all-gather.14.cloned.1.call-start = ((), (), s32[]{:S(2)}) async-start(), calls=%async_computation.7 | async-start | bytes 2359296 | tf_op jit(solution)/shard_map/all_gather | solution.py:69
  536.7 5.4 copy-start.2
Sparse Core Ops, SparseCore 0:
  8.9 83.4 all-gather.5
  94.0 79.2 all-gather.7
  174.8 44.1 all-gather.9
  222.1 79.5 all-reduce.5
  303.5 37.3 all-gather.11
  351.3 86.1 all-reduce.3
  456.8 50.1 reduce-scatter.1
  508.9 27.7 all-gather.13
where the time goes:
time: 552 us
  waiting for transfers between devices  447 us (81%)
  matrix products  59.6 us (11%)
  blocking collectives  25.6 us (5%)
  between operations  13.6 us (2%)
    psum x1, waiting for transfers between devices, local(): rotated = lax.psum(partial_value, 'feat')  85.9 us
    all_gather x1, waiting for transfers between devices, local(): piece_g = lax.all_gather(grad_out, 'feat', axis=1, tiled=True)  83.6 us
    psum x1, waiting for transfers between devices, local(): lax.psum((cross_one, cross_two, sum_x, sum_g), 'rows')  82.8 us
    all_gather x1, waiting for transfers between devices, local(): piece_x = lax.all_gather(features, 'feat', axis=1, tiled=True)  74 us
    reduce_scatter x1, waiting for transfers between devices, local(): lax.psum_scatter(lax.dot_general(back_rot, basis_cols, contract_last, pre...  50 us
    all_gather x1, waiting for transfers between devices, local(): basis_block = lax.all_gather(eigvecs, 'rows', axis=1, tiled=True)  32.3 us
    all_gather x1, waiting for transfers between devices, local(): sens_scaled = lax.all_gather(scaled_own, 'rows', axis=0, tiled=True)  27.9 us
    psum x1, blocking collectives, local(): lax.psum((cross_one, cross_two, sum_x, sum_g), 'rows')  25.6 us
  transfers between devices with their start and end apart: 8, of which 8 were waited for; matrix products, arithmetic and copies ran while one was open for 5% of the time, Pallas kernels for 0%

commit v1 on v0

--- a/solution.py
+++ b/solution.py
@@ -54,7 +54,9 @@
     narrow = basis_cols.shape[1]
     inner_prod = jnp.dot(sym_gram, basis_cols, precision=highest)
     partial_value = lax.dot_general(basis_block, inner_prod, contract_rows, precision=highest)
-    rotated = lax.psum(partial_value, "feat")
+    rotated = partial_value
+    for hop in (1, 2):
+        rotated = rotated + lax.ppermute(rotated, "feat", [(dev, dev ^ hop) for dev in range(4)])
     first_col = lax.axis_index("rows") * narrow
     lam_col = lax.dynamic_slice_in_dim(eigvals, first_col, narrow)
     scaled = divided(eigvals, lam_col, first_col) * rotated

time: 552 us -> 603 us (1.092)
  waiting for transfers between devices: 447 us -> 499 us
  matrix products: 59.6 us -> 52.5 us
    ppermute x0 -> x2, waiting for transfers between devices: none -> 137 us  [local(): lax.ppermute(rotated, 'feat', [(dev, dev ^ hop) for dev in range(4)])]
    psum x1 -> x0, waiting for transfers between devices: 85.9 us -> none  [local(): rotated = lax.psum(partial_value, 'feat')]
  transfers between devices with their start and end apart: 8 -> 9, of which waited for: 8 -> 9; matrix products, arithmetic and copies ran while one was open for 5% -> 4% of each run, Pallas kernels for 0% -> 0%
where the time goes in v1:
time: 603 us; the launch traced here: 602 us
  waiting for transfers between devices  499 us (83%)
  matrix products  52.5 us (9%)
  blocking collectives  25.6 us (4%)
  between operations  13.6 us (2%)
  other arithmetic  7.02 us (1%)
    ppermute x2, waiting for transfers between devices, local(): lax.ppermute(rotated, 'feat', [(dev, dev ^ hop) for dev in range(4)])  137 us
    all_gather x1, waiting for transfers between devices, local(): piece_g = lax.all_gather(grad_out, 'feat', axis=1, tiled=True)  83.6 us
    psum x1, waiting for transfers between devices, local(): lax.psum((cross_one, cross_two, sum_x, sum_g), 'rows')  82.8 us
    all_gather x1, waiting for transfers between devices, local(): piece_x = lax.all_gather(features, 'feat', axis=1, tiled=True)  74 us
    reduce_scatter x1, waiting for transfers between devices, local(): lax.psum_scatter(lax.dot_general(back_rot, basis_cols, contract_last, pre...  51 us
    all_gather x1, waiting for transfers between devices, local(): basis_block = lax.all_gather(eigvecs, 'rows', axis=1, tiled=True)  32.3 us
    all_gather x1, waiting for transfers between devices, local(): sens_scaled = lax.all_gather(scaled_own, 'rows', axis=0, tiled=True)  27.9 us
    psum x1, blocking collectives, local(): lax.psum((cross_one, cross_two, sum_x, sum_g), 'rows')  25.6 us
  transfers between devices with their start and end apart: 9, of which 9 were waited for; matrix products, arithmetic and copies ran while one was open for 4% of the time, Pallas kernels for 0%

profile of v1, /device:TPU:0, one launch (start us, length us, event | category | flops | bytes accessed | tf_op | source)
XLA Modules:
  0.0 602.4 jit_solution(4534480307677139721)
XLA Ops:
  6.5 0.7 all-gather.6.cloned.1.call-update
  8.8 83.6 %all-gather.6.cloned.1.call-done = bf16[1024,2048]{1,0:T(8,128)(2,1)} async-done(((bf16[1024,512]{1,0:T(8,128)(2,1)}), bf16[1024,2048]{1,0:T(8,128)(2,1)}) %all-gather.6.cloned.1.call-update) | async-done | bytes 4194320 | tf_op jit(solution)/shard_map/all_gather | solution.py:73
  92.4 6.8 %fusion.41 = f32[512,2048]{1,0:T(8,128)} fusion(bf16[1024,512]{1,0:T(8,128)(2,1)} %param.5, bf16[1024,2048]{1,0:T(8,128)(2,1)} %all-gather.6.cloned.1.call-done), kind=kOutput, calls=%fused_computation.52 | convolution fusion | flops 2147483648 | bytes 9437184 | tf_op jit(solution)/shard_map/dot_general | solution.py:29
  99.2 74.0 %all-gather.8.cloned.1.call-done = bf16[1024,2048]{1,0:T(8,128)(2,1)} async-done(((bf16[1024,512]{1,0:T(8,128)(2,1)}), bf16[1024,2048]{1,0:T(8,128)(2,1)}) %all-gather.8.cloned.1.call-update) | async-done | bytes 4194320 | tf_op jit(solution)/shard_map/all_gather | solution.py:72
  173.2 7.8 %convolution_add_fusion = f32[512,2048]{1,0:T(8,128)} fusion(f32[512,2048]{1,0:T(8,128)} %fusion.41, bf16[1024,512]{1,0:T(8,128)(2,1)S(1)} %copy-done.3, bf16[1024,2048]{1,0:T(8,128)(2,1)} %all-gather.8.cloned.1.call-done), kind=kOutput, calls=%fused_computation.17 | convolution fusion | flops 2148532224 | bytes 13631488 | tf_op jit(solution)/shard_map/dot_general | solution.py:32
  181.7 3.0 convert_reduce_fusion
  185.8 25.6 %all-reduce = (f32[2048]{0:T(1024)S(1)}, f32[2048]{0:T(1024)S(1)}) all-reduce(f32[2048]{0:T(1024)S(1)} %convert_reduce_fusion, f32[2048]{0:T(1024)S(1)} %convert_reduce_fusion.1), channel_id=1, replica_groups=mesh['rows'=8,'feat'=4] {'rows'}, use_global_device_ids=true, to_apply=%region_3.0 | all-reduce | flops 4096 | bytes 32768 | tf_op jit(solution)/shard_map/psum | solution.py:40
  211.6 7.4 %all-gather.10.cloned.1.call-done = f32[2048,256]{1,0:T(8,128)} async-done(((f32[512,256]{1,0:T(8,128)}), f32[2048,256]{1,0:T(8,128)}) %all-gather.10.cloned.1.call-update) | async-done | bytes 2097168 | tf_op jit(solution)/shard_map/all_gather | solution.py:52
  219.0 82.8 %all-reduce.3.cloned.1.call-done = f32[512,2048]{1,0:T(8,128)} async-done(((f32[512,2048]{1,0:T(8,128)}), f32[512,2048]{1,0:T(8,128)}) %all-reduce.3.cloned.1.call-update) | async-done | bytes 4194320 | tf_op jit(solution)/shard_map/psum | solution.py:40
  301.7 6.9 %fusion.6 = f32[512,256]{1,0:T(8,128)S(1)} fusion(f32[2048,256]{1,0:T(8,128)} %all-gather.10.cloned.1.call-done, f32[512,2048]{1,0:T(8,128)} %all-reduce.3.cloned.1.call-done, f32[2048]{0:T(1024)S(1)} %get-tuple-element.11, f32[512]{0:T(512)S(1)} %dynamic_slice.11, f32[2048]{0:T(1024)S(1)} %get-tuple-element.12, f32[512]{0:T(512)S(1)} %dynamic_slice.10), kind=kOutput, calls=%fused_computation.8 | convolution fusion | flops 3227516928 | bytes 6836224 | tf_op jit(solution)/shard_map/dot_general | solution.py:55
  308.6 32.3 %all-gather.12.cloned.1.call-done = f32[512,2048]{1,0:T(8,128)} async-done(((f32[512,256]{1,0:T(8,128)}), f32[512,2048]{1,0:T(8,128)}) %all-gather.12.cloned.1.call-update) | async-done | bytes 4194320 | tf_op jit(solution)/shard_map/all_gather | solution.py:53
  340.9 5.4 convolution_bitcast_fusion
  346.3 1.6 collective-permute-start
  347.9 46.3 %collective-permute-done = f32[2048,256]{0,1:T(8,128)S(1)} collective-permute-done((f32[2048,256]{0,1:T(8,128)S(1)}, f32[2048,256]{0,1:T(8,128)S(1)}, u32[]{:S(2)}, u32[]{:S(2)}) %collective-permute-start) | collective-permute-done | bytes 2097184 | tf_op jit(solution)/shard_map/ppermute | solution.py:59
  394.2 1.6 add.54
  395.7 2.4 collective-permute-start.1
  398.2 90.6 %collective-permute-done.1 = f32[2048,256]{0,1:T(8,128)} collective-permute-done((f32[2048,256]{0,1:T(8,128)}, f32[2048,256]{0,1:T(8,128)}, u32[]{:S(2)}, u32[]{:S(2)}) %collective-permute-start.1) | collective-permute-done | bytes 2097184 | tf_op jit(solution)/shard_map/ppermute | solution.py:59
  488.8 8.4 %fusion.15 = f32[256,512]{1,0:T(8,128)S(1)} fusion(f32[512,2048]{1,0:T(8,128)} %all-gather.12.cloned.1.call-done, f32[2048,256]{0,1:T(8,128)} %add.54, f32[2048,256]{0,1:T(8,128)} %collective-permute-done.1, f32[256]{0:T(256)S(1)} %get-tuple-element.8, f32[2048]{0:T(1024)S(1)} %copy-done.5, f32[256]{0:T(256)S(1)} %get-tuple-element.7, ...), kind=kOutput, calls=%fused_computation.20 | convolution fusion | flops 3225419776 | bytes 8940544 | tf_op jit(solution)/shard_map/dot_general | solution.py:63
  497.2 8.6 %fusion.42 = f32[512,2048]{1,0:T(8,128)} fusion(f32[256,512]{1,0:T(8,128)S(1)} %fusion.15, f32[2048,256]{1,0:T(8,128)S(1)} %copy-done.4), kind=kOutput, calls=%fused_computation.53 | convolution fusion | flops 3221225472 | bytes 6815744 | tf_op jit(solution)/shard_map/dot_general | solution.py:65
  506.1 51.0 %reduce-scatter.2.cloned.1.call-done = f32[64,2048]{1,0:T(8,128)} async-done(((f32[512,2048]{1,0:T(8,128)}), f32[64,2048]{1,0:T(8,128)}) %reduce-scatter.2.cloned.1.call-update) | async-done | bytes 524304 | tf_op jit(solution)/shard_map/reduce_scatter | solution.py:64
  557.1 1.8 multiply_convert_fusion
  558.9 27.9 %all-gather.14.cloned.1.call-done = bf16[512,2048]{1,0:T(8,128)(2,1)} async-done(((bf16[64,2048]{1,0:T(8,128)(2,1)}), bf16[512,2048]{1,0:T(8,128)(2,1)}) %all-gather.14.cloned.1.call-update) | async-done | bytes 2097168 | tf_op jit(solution)/shard_map/all_gather | solution.py:71
  586.8 5.4 fusion.2
  592.2 3.3 add_convert_fusion
  (32 shorter events, 3.8 us)
Async XLA Ops:
  6.5 585.7 %copy-start = (bf16[2048,512]{1,0:T(8,128)(2,1)S(1)}, bf16[2048,512]{1,0:T(8,128)(2,1)}, u32[]{:S(2)}) copy-start(bf16[2048,512]{1,0:T(8,128)(2,1)} %param.9) | copy-start | bytes 6291460
  6.5 85.9 %all-gather.6.cloned.1.call-start = ((), (), s32[]{:S(2)}) async-start(), calls=%async_computation.1 | async-start | bytes 5242880 | tf_op jit(solution)/shard_map/all_gather | solution.py:73
  7.3 166.0 %all-gather.8.cloned.1.call-start = ((), (), s32[]{:S(2)}) async-start(), calls=%async_computation.2 | async-start | bytes 5242880 | tf_op jit(solution)/shard_map/all_gather | solution.py:72
  8.0 211.0 %all-gather.10.cloned.1.call-start = ((), (), s32[]{:S(2)}) async-start(), calls=%async_computation.3 | async-start | bytes 2621440 | tf_op jit(solution)/shard_map/all_gather | solution.py:52
  8.7 164.5 %copy-start.3 = (bf16[1024,512]{1,0:T(8,128)(2,1)S(1)}, bf16[1024,512]{1,0:T(8,128)(2,1)}, u32[]{:S(2)}) copy-start(bf16[1024,512]{1,0:T(8,128)(2,1)} %param.6) | copy-start | bytes 3145732
  8.8 293.0 %all-reduce.3.cloned.1.call-start = ((), (), s32[]{:S(2)}) async-start(), calls=%async_computation.7 | async-start | bytes 8388608 | tf_op jit(solution)/shard_map/psum | solution.py:40
  181.1 159.9 %all-gather.12.cloned.1.call-start = ((), (), s32[]{:S(2)}) async-start(), calls=%async_computation.4 | async-start | bytes 4718592 | tf_op jit(solution)/shard_map/all_gather | solution.py:53
  181.6 375.4 %reduce-scatter.2.cloned.1.call-start = ((), (), s32[]{:S(2)}) async-start(), calls=%async_computation.5 | async-start | bytes 4718592 | tf_op jit(solution)/shard_map/reduce_scatter | solution.py:64
  181.7 3.5 copy-start.1
  346.3 51.9 %copy-start.5 = (f32[2048]{0:T(1024)S(1)}, f32[2048]{0:T(1024)}, u32[]{:S(2)}) copy-start(f32[2048]{0:T(1024)} %param.8) | copy-start | bytes 24580
  346.3 47.9 %collective-permute-start = (f32[2048,256]{0,1:T(8,128)S(1)}, f32[2048,256]{0,1:T(8,128)S(1)}, u32[]{:S(2)}, u32[]{:S(2)}) collective-permute-start(f32[2048,256]{0,1:T(8,128)S(1)} %convolution_bitcast_fusion), channel_id=1, source_target_pairs={{0,1},{1,0},{2,3},{3,2},{4,5},{5,4},{6,7},{7,6},{8,9},{9,8},{10,11... | collective-permute-start | bytes 6291464 | tf_op jit(solution)/shard_map/ppermute | solution.py:59
  395.7 93.1 %collective-permute-start.1 = (f32[2048,256]{0,1:T(8,128)}, f32[2048,256]{0,1:T(8,128)}, u32[]{:S(2)}, u32[]{:S(2)}) collective-permute-start(f32[2048,256]{0,1:T(8,128)} %add.54), channel_id=1, source_target_pairs={{0,2},{1,3},{2,0},{3,1},{4,6},{5,7},{6,4},{7,5},{8,10},{9,11},{10,... | collective-permute-start | bytes 6291464 | tf_op jit(solution)/shard_map/ppermute | solution.py:59
  488.8 8.4 %copy-start.4 = (f32[2048,256]{1,0:T(8,128)S(1)}, f32[2048,256]{1,0:T(8,128)}, u32[]{:S(2)}) copy-start(f32[2048,256]{1,0:T(8,128)} %all-gather.10.cloned.1.call-done) | copy-start | bytes 6291460
  505.8 81.0 %all-gather.14.cloned.1.call-start = ((), (), s32[]{:S(2)}) async-start(), calls=%async_computation.6 | async-start | bytes 2359296 | tf_op jit(solution)/shard_map/all_gather | solution.py:71
  586.8 5.4 copy-start.2
Sparse Core Ops, SparseCore 0:
  8.9 83.4 all-gather.5
  94.0 79.2 all-gather.7
  174.8 44.1 all-gather.9
  222.1 79.5 all-reduce.2
  303.5 37.3 all-gather.11
  505.9 51.0 reduce-scatter.1
  559.0 27.7 all-gather.13
